TPU v7x, 32 devices: a whole 2x2x4 slice. The times are simulated.
32 devices in a mesh: section: 2 (over x), dp: 8 (over z, y), mp: 2 (over core).
Axes of the slice: x: 2, y: 2, z: 4, core: 2. Of those that a mesh axis runs over, the one named last changes fastest.
Arguments:
- layer_inputs: bfloat16 [2, 128, 4096], P('section', None, 'mp'), may hold values from -6 to 6
- pre_act: bfloat16 [2, 128, 8192], P('section', None, 'dp'), may hold values from -6 to 6
- out_grad: bfloat16 [128, 4096], P(None, 'mp'), may hold values from -4 to 4
- w_in: bfloat16 [8, 2, 512, 4096], P('dp', 'section', None, 'mp'), may hold values from -0.09375 to 0.09375
- w_out: bfloat16 [8, 2, 512, 4096], P('dp', 'section', None, 'mp'), may hold values from -0.0625 to 0.0625
Outputs:
- in_grads: bfloat16 [2, 128, 4096], P('section', None, 'mp')
- grad_in: float32 [8, 2, 512, 4096], P('dp', 'section', None, 'mp')
- grad_out: float32 [8, 2, 512, 4096], P('dp', 'section', None, 'mp')
All inputs are finite; a program needn't handle non-finite values.
Results may differ from a plain program's by a relative error of at most 0.035.
Values may be sent and summed in bfloat16 or wider, within the bound.
A program may use at most 64 MiB of HBM per device.

v0:
```python
import jax
import jax.numpy as jnp
from jax import lax
from jax.sharding import PartitionSpec as P

MICRO = 2


def shifted(value, axis, by):
    size = lax.axis_size(axis)
    pairs = [(i, i + by) for i in range(size) if 0 <= i + by < size]
    return lax.ppermute(value, axis, pairs)


def gelu_slope(value):
    cdf = 0.5 * (1.0 + lax.erf(value * 0.7071067811865476))
    dens = jnp.exp(-0.5 * value * value) * 0.3989422804014327
    return cdf + value * dens


def rounded(value):
    return lax.optimization_barrier(value.astype(jnp.bfloat16)).astype(jnp.float32)


def by_tokens(left, right):
    return lax.dot_general(
        left, right, (((0,), (0,)), ((), ())), preferred_element_type=jnp.float32
    )


def body(layer_inputs, pre_act, out_grad, w_in, w_out):
    sections = lax.axis_size("section")
    spot = lax.axis_index("section")
    tok_rows = out_grad.shape[0]
    block = tok_rows // MICRO
    width = out_grad.shape[1]
    full_in, full_out = (
        lax.all_gather(w_in, "section", axis=1, tiled=True),
        lax.all_gather(w_out, "section", axis=1, tiled=True),
    )
    units = full_in.shape[1] * full_in.shape[2]
    per_block = full_in.shape[2]
    in_rows = full_in.reshape(units, width)
    out_rows = full_out.reshape(units, width)
    inputs = layer_inputs[0]
    saved = pre_act[0]
    is_last = spot == sections - 1

    def advance(step, state):
        incoming, dys, gees, results = state
        micro_id = step - (sections - 1 - spot)
        valid = jnp.logical_and(micro_id >= 0, micro_id < MICRO)
        begin = jnp.clip(micro_id, 0, MICRO - 1) * block
        given = lax.dynamic_slice_in_dim(out_grad, begin, block, 0)
        upper = jnp.where(is_last, given, incoming)
        partial_value = lax.dot_general(
            upper, out_rows, (((1,), (1,)), ((), ())), preferred_element_type=jnp.float32
        )
        summed = lax.psum(partial_value.astype(jnp.bfloat16), "mp").astype(jnp.float32)
        rows_pre = lax.dynamic_slice_in_dim(saved, begin, block, 0).astype(jnp.float32)
        gee = (summed * gelu_slope(rows_pre)).astype(jnp.bfloat16)
        branch = jnp.dot(gee, in_rows, preferred_element_type=jnp.float32)
        total = lax.psum(branch.astype(jnp.bfloat16), "dp").astype(jnp.float32)
        result = (upper.astype(jnp.float32) + total).astype(jnp.bfloat16)
        outgoing = shifted(result, "section", -1)
        old_dy = lax.dynamic_slice_in_dim(dys, begin, block, 0)
        old_gee = lax.dynamic_slice_in_dim(gees, begin, block, 0)
        old_res = lax.dynamic_slice_in_dim(results, begin, block, 0)
        dys = lax.dynamic_update_slice_in_dim(dys, jnp.where(valid, upper, old_dy), begin, 0)
        gees = lax.dynamic_update_slice_in_dim(gees, jnp.where(valid, gee, old_gee), begin, 0)
        results = lax.dynamic_update_slice_in_dim(
            results, jnp.where(valid, result, old_res), begin, 0
        )
        return (outgoing, dys, gees, results)

    start_state = (
        jnp.zeros((block, width), jnp.bfloat16),
        jnp.zeros((tok_rows, width), jnp.bfloat16),
        jnp.zeros((tok_rows, units), jnp.bfloat16),
        jnp.zeros((tok_rows, width), jnp.bfloat16),
    )
    final_state = lax.fori_loop(0, sections + MICRO - 1, advance, start_state)
    dys = final_state[1]
    gees = final_state[2]
    results = final_state[3]
    hidden = jax.nn.gelu(saved.astype(jnp.float32), approximate=False).astype(jnp.bfloat16)
    offset = spot * per_block
    empty = jnp.zeros((per_block, width), jnp.float32)
    piece = (
        lax.all_gather(inputs[None], "section", axis=0, tiled=True),
        lax.all_gather(dys[None], "section", axis=0, tiled=True),
        lax.all_gather(gees[None], "section", axis=0, tiled=True),
        lax.all_gather(hidden[None], "section", axis=0, tiled=True),
    )
    acc_in = empty
    acc_out = empty
    for row in range(piece[0].shape[0]):
        gee_cols = lax.dynamic_slice_in_dim(piece[2][row], offset, per_block, 1)
        hid_cols = lax.dynamic_slice_in_dim(piece[3][row], offset, per_block, 1)
        acc_in = acc_in + rounded(by_tokens(gee_cols, piece[0][row]))
        acc_out = acc_out + rounded(by_tokens(hid_cols, piece[1][row]))
    acc_in, acc_out = (acc_in, acc_out)
    grad_in = acc_in.reshape(1, 1, per_block, width)
    grad_out = acc_out.reshape(1, 1, per_block, width)
    return (results[None], grad_in, grad_out)


def solution(mesh):
    in_specs = (
        P("section", None, "mp"),
        P("section", None, "dp"),
        P(None, "mp"),
        P("dp", "section", None, "mp"),
        P("dp", "section", None, "mp"),
    )
    out_specs = (
        P("section", None, "mp"),
        P("dp", "section", None, "mp"),
        P("dp", "section", None, "mp"),
    )
    return jax.shard_map(body, mesh=mesh, in_specs=in_specs, out_specs=out_specs, check_vma=False)
```

profile of v0, /device:TPU:0, one launch (start us, length us, event | category | flops | bytes accessed | tf_op | source)
XLA Modules:
  0.0 509.6 jit_solution(17135875296356808804)
XLA Ops:
  7.2 0.0 copy-start.4
  7.2 0.0 copy-start.2
  7.2 0.0 all-gather.7.cloned.1.call-start
  7.2 0.7 all-gather.7.cloned.1.call-update
  7.9 0.0 all-gather.9.cloned.1.call-start
  8.0 0.7 all-gather.9.cloned.1.call-update
  8.7 60.3 %all-gather.7.cloned.1.call-done = bf16[1,2,512,2048]{3,2,0,1:T(8,128)(2,1)} async-done(((bf16[1,1,512,2048]{3,2,0,1:T(8,128)(2,1)}), bf16[1,2,512,2048]{3,2,0,1:T(8,128)(2,1)}) %all-gather.7.cloned.1.call-update) | async-done | bytes 4194320 | tf_op jit(solution)/shard_map/all_gather | solution.py:39
  69.0 58.3 %all-gather.9.cloned.1.call-done = bf16[1,2,512,2048]{3,2,0,1:T(8,128)(2,1)} async-done(((bf16[1,1,512,2048]{3,2,0,1:T(8,128)(2,1)}), bf16[1,2,512,2048]{3,2,0,1:T(8,128)(2,1)}) %all-gather.9.cloned.1.call-update) | async-done | bytes 4194320 | tf_op jit(solution)/shard_map/all_gather | solution.py:38
  127.5 0.0 copy-done.4
  127.5 0.0 copy-done.2
  127.5 320.8 %while.21 = (s32[]{:T(128)}, bf16[64,2048]{1,0:T(8,128)(2,1)S(1)}, bf16[128,2048]{1,0:T(8,128)(2,1)S(1)}, bf16[128,1024]{1,0:T(8,128)(2,1)S(1)}, bf16[128,2048]{...) while((s32[]{:T(128)}, bf16[64,2048]{1,0:T(8,128)(2,1)S(1)}, ...), condition=%wide.region_3.4_spmd, body=%wide.region_0.3_spmd.sunk | while | flops 539820032 | bytes 16384420 | solution.py:82
  127.5 0.0 all-reduce.3.cloned.1.call-start
  127.6 0.1 select_dynamic-update-slice_fusion.6
  127.7 4.2 convolution_convert_fusion.8
  131.9 0.0 all-reduce.3.cloned.1.call-update
  132.0 0.0 all-reduce.5.cloned.1.call-start
  132.0 18.0 %all-reduce.3.cloned.1.call-done = bf16[64,1024]{1,0:T(8,128)(2,1)} async-done(((bf16[64,1024]{1,0:T(8,128)(2,1)}), bf16[64,1024]{1,0:T(8,128)(2,1)}) %all-reduce.3.cloned.1.call-update) | async-done | bytes 131088 | tf_op jit(solution)/shard_map/while/body/eval_jaxpr/psum | solution.py:59
  150.0 3.9 convolution_convert_fusion.9
  153.9 0.0 all-reduce.5.cloned.1.call-update
  153.9 72.4 %all-reduce.5.cloned.1.call-done = bf16[64,2048]{1,0:T(8,128)(2,1)} async-done(((bf16[64,2048]{1,0:T(8,128)(2,1)}), bf16[64,2048]{1,0:T(8,128)(2,1)}) %all-reduce.5.cloned.1.call-update) | async-done | bytes 262160 | tf_op jit(solution)/shard_map/while/body/eval_jaxpr/psum | solution.py:63
  226.3 1.1 select_dynamic-update-slice_fusion.7
  227.3 1.3 collective-permute-start
  228.6 0.0 copy-done
  228.7 0.2 select_dynamic-update-slice_fusion.8
  228.8 6.8 %collective-permute-done = bf16[64,2048]{1,0:T(8,128)(2,1)S(1)} collective-permute-done((bf16[64,2048]{1,0:T(8,128)(2,1)S(1)}, bf16[64,2048]{1,0:T(8,128)(2,1)S(1)}, u32[]{:S(2)}, u32[]{:S(2)}) %collective-permute-start) | collective-permute-done | bytes 262176 | tf_op jit(solution)/shard_map/while/body/eval_jaxpr/ppermute | solution.py:12
  235.6 0.1 select_dynamic-update-slice_fusion.6
  235.7 4.2 convolution_convert_fusion.8
  240.0 0.0 all-reduce.3.cloned.1.call-update
  240.0 0.0 all-reduce.5.cloned.1.call-start
  240.1 16.3 %all-reduce.3.cloned.1.call-done = bf16[64,1024]{1,0:T(8,128)(2,1)} async-done(((bf16[64,1024]{1,0:T(8,128)(2,1)}), bf16[64,1024]{1,0:T(8,128)(2,1)}) %all-reduce.3.cloned.1.call-update) | async-done | bytes 131088 | tf_op jit(solution)/shard_map/while/body/eval_jaxpr/psum | solution.py:59
  256.4 3.9 convolution_convert_fusion.9
  260.2 0.0 all-reduce.5.cloned.1.call-update
  260.3 72.4 %all-reduce.5.cloned.1.call-done = bf16[64,2048]{1,0:T(8,128)(2,1)} async-done(((bf16[64,2048]{1,0:T(8,128)(2,1)}), bf16[64,2048]{1,0:T(8,128)(2,1)}) %all-reduce.5.cloned.1.call-update) | async-done | bytes 262160 | tf_op jit(solution)/shard_map/while/body/eval_jaxpr/psum | solution.py:63
  332.6 1.1 select_dynamic-update-slice_fusion.7
  333.7 1.3 collective-permute-start
  335.0 0.2 select_dynamic-update-slice_fusion.8
  335.2 6.8 %collective-permute-done = bf16[64,2048]{1,0:T(8,128)(2,1)S(1)} collective-permute-done((bf16[64,2048]{1,0:T(8,128)(2,1)S(1)}, bf16[64,2048]{1,0:T(8,128)(2,1)S(1)}, u32[]{:S(2)}, u32[]{:S(2)}) %collective-permute-start) | collective-permute-done | bytes 262176 | tf_op jit(solution)/shard_map/while/body/eval_jaxpr/ppermute | solution.py:12
  342.0 0.0 all-reduce.3.cloned.1.call-start
  342.0 0.1 select_dynamic-update-slice_fusion.6
  342.1 4.2 convolution_convert_fusion.8
  346.4 0.0 all-reduce.3.cloned.1.call-update
  346.4 0.0 all-reduce.5.cloned.1.call-start
  346.4 16.3 %all-reduce.3.cloned.1.call-done = bf16[64,1024]{1,0:T(8,128)(2,1)} async-done(((bf16[64,1024]{1,0:T(8,128)(2,1)}), bf16[64,1024]{1,0:T(8,128)(2,1)}) %all-reduce.3.cloned.1.call-update) | async-done | bytes 131088 | tf_op jit(solution)/shard_map/while/body/eval_jaxpr/psum | solution.py:59
  362.7 3.9 convolution_convert_fusion.9
  366.6 0.0 all-reduce.5.cloned.1.call-update
  366.6 72.4 %all-reduce.5.cloned.1.call-done = bf16[64,2048]{1,0:T(8,128)(2,1)} async-done(((bf16[64,2048]{1,0:T(8,128)(2,1)}), bf16[64,2048]{1,0:T(8,128)(2,1)}) %all-reduce.5.cloned.1.call-update) | async-done | bytes 262160 | tf_op jit(solution)/shard_map/while/body/eval_jaxpr/psum | solution.py:63
  439.0 1.1 select_dynamic-update-slice_fusion.7
  440.1 1.3 collective-permute-start
  441.4 0.2 select_dynamic-update-slice_fusion.8
  441.5 6.8 %collective-permute-done = bf16[64,2048]{1,0:T(8,128)(2,1)S(1)} collective-permute-done((bf16[64,2048]{1,0:T(8,128)(2,1)S(1)}, bf16[64,2048]{1,0:T(8,128)(2,1)S(1)}, u32[]{:S(2)}, u32[]{:S(2)}) %collective-permute-start) | collective-permute-done | bytes 262176 | tf_op jit(solution)/shard_map/while/body/eval_jaxpr/ppermute | solution.py:12
  448.3 0.7 all-gather.11.cloned.1.call-update
  449.1 0.0 all-gather.13.cloned.1.call-start
  449.1 1.1 fusion.10
  450.2 8.1 %all_gather.22 = bf16[2,128,1024]{2,1,0:T(8,128)(2,1)S(1)} all-gather(bf16[1,128,1024]{2,1,0:T(8,128)(2,1)S(1)} %fusion.10), channel_id=1, replica_groups=mesh['section'=2,'dp'=8,'mp'=2] {'section'}, dimensions={0}, use_global_device_ids=true | all-gather | bytes 786432 | tf_op jit(solution)/shard_map/all_gather | solution.py:93
  458.3 12.7 %all-gather = bf16[256,1024]{1,0:T(8,128)(2,1)S(1)} all-gather(bf16[128,1024]{1,0:T(8,128)(2,1)S(1)} %get-tuple-element.260), channel_id=2, replica_groups=mesh['section'=2,'dp'=8,'mp'=2] {'section'}, dimensions={0}, use_global_device_ids=true | all-gather | bytes 786432 | tf_op jit(solution)/shard_map/all_gather | solution.py:92
  471.0 0.0 all-gather.13.cloned.1.call-update
  471.1 3.3 all-gather.11.cloned.1.call-done
  474.4 1.8 convolution_convert_fusion.4
  476.2 1.8 convolution_convert_fusion.5
  478.0 2.8 add_bitcast_fusion.1
  480.8 15.6 %all-gather.13.cloned.1.call-done = bf16[256,2048]{1,0:T(8,128)(2,1)} async-done(((bf16[128,2048]{1,0:T(8,128)(2,1)}), bf16[256,2048]{1,0:T(8,128)(2,1)}) %all-gather.13.cloned.1.call-update) | async-done | bytes 1048592 | tf_op jit(solution)/shard_map/all_gather | solution.py:91
  496.4 1.8 convolution_convert_fusion.2
  498.1 1.8 convolution_convert_fusion.3
  499.9 2.8 add_bitcast_fusion
  (17 shorter events, 0.2 us)
Async XLA Ops:
  7.2 120.3 %copy-start.4 = (bf16[128,2048]{1,0:T(8,128)(2,1)S(1)}, bf16[128,2048]{1,0:T(8,128)(2,1)}, u32[]{:S(2)}) copy-start(bf16[128,2048]{1,0:T(8,128)(2,1)} %param.9) | copy-start | bytes 1572868
  7.2 120.3 %copy-start.2 = (bf16[1,128,1024]{2,1,0:T(8,128)(2,1)S(1)}, bf16[1,128,1024]{2,1,0:T(8,128)(2,1)}, u32[]{:S(2)}) copy-start(bf16[1,128,1024]{2,1,0:T(8,128)(2,1)} %param.8) | copy-start | bytes 786436
  7.2 61.8 %all-gather.7.cloned.1.call-start = ((), (), s32[]{:S(2)}) async-start(), calls=%async_computation | async-start | bytes 6291456 | tf_op jit(solution)/shard_map/all_gather | solution.py:39
  7.9 119.4 %all-gather.9.cloned.1.call-start = ((), (), s32[]{:S(2)}) async-start(), calls=%async_computation.1 | async-start | bytes 6291456 | tf_op jit(solution)/shard_map/all_gather | solution.py:38
  127.5 22.5 %all-reduce.3.cloned.1.call-start = ((), (), s32[]{:S(2)}) async-start(), calls=%async_computation.4 | async-start | bytes 262144 | tf_op jit(solution)/shard_map/while/body/eval_jaxpr/psum | solution.py:59
  132.0 94.3 %all-reduce.5.cloned.1.call-start = ((), (), s32[]{:S(2)}) async-start(), calls=%async_computation.5 | async-start | bytes 524288 | tf_op jit(solution)/shard_map/while/body/eval_jaxpr/psum | solution.py:63
  150.0 78.6 %copy-start = (bf16[64,1024]{1,0:T(8,128)(2,1)S(1)}, bf16[64,1024]{1,0:T(8,128)(2,1)}, u32[]{:S(2)}) copy-start(bf16[64,1024]{1,0:T(8,128)(2,1)} %all-reduce.3.cloned.1.call-done) | copy-start | bytes 393220 | tf_op jit(solution)/shard_map/while
  227.3 8.3 %collective-permute-start = (bf16[64,2048]{1,0:T(8,128)(2,1)S(1)}, bf16[64,2048]{1,0:T(8,128)(2,1)S(1)}, u32[]{:S(2)}, u32[]{:S(2)}) collective-permute-start(bf16[64,2048]{1,0:T(8,128)(2,1)S(1)} %get-tuple-element.364), channel_id=1, source_target_pairs={{16,0},{17,1},{18,2},{19,3},{20,4},{21,5},{22,6},{23,7},{24,8},{25... | collective-permute-start | bytes 786440 | tf_op jit(solution)/shard_map/while/body/eval_jaxpr/ppermute | solution.py:12
  235.6 20.8 %all-reduce.3.cloned.1.call-start = ((), (), s32[]{:S(2)}) async-start(), calls=%async_computation.4 | async-start | bytes 262144 | tf_op jit(solution)/shard_map/while/body/eval_jaxpr/psum | solution.py:59
  240.0 92.6 %all-reduce.5.cloned.1.call-start = ((), (), s32[]{:S(2)}) async-start(), calls=%async_computation.5 | async-start | bytes 524288 | tf_op jit(solution)/shard_map/while/body/eval_jaxpr/psum | solution.py:63
  256.4 78.6 %copy-start = (bf16[64,1024]{1,0:T(8,128)(2,1)S(1)}, bf16[64,1024]{1,0:T(8,128)(2,1)}, u32[]{:S(2)}) copy-start(bf16[64,1024]{1,0:T(8,128)(2,1)} %all-reduce.3.cloned.1.call-done) | copy-start | bytes 393220 | tf_op jit(solution)/shard_map/while
  333.7 8.3 %collective-permute-start = (bf16[64,2048]{1,0:T(8,128)(2,1)S(1)}, bf16[64,2048]{1,0:T(8,128)(2,1)S(1)}, u32[]{:S(2)}, u32[]{:S(2)}) collective-permute-start(bf16[64,2048]{1,0:T(8,128)(2,1)S(1)} %get-tuple-element.364), channel_id=1, source_target_pairs={{16,0},{17,1},{18,2},{19,3},{20,4},{21,5},{22,6},{23,7},{24,8},{25... | collective-permute-start | bytes 786440 | tf_op jit(solution)/shard_map/while/body/eval_jaxpr/ppermute | solution.py:12
  342.0 20.8 %all-reduce.3.cloned.1.call-start = ((), (), s32[]{:S(2)}) async-start(), calls=%async_computation.4 | async-start | bytes 262144 | tf_op jit(solution)/shard_map/while/body/eval_jaxpr/psum | solution.py:59
  346.4 92.6 %all-reduce.5.cloned.1.call-start = ((), (), s32[]{:S(2)}) async-start(), calls=%async_computation.5 | async-start | bytes 524288 | tf_op jit(solution)/shard_map/while/body/eval_jaxpr/psum | solution.py:63
  362.7 78.6 %copy-start = (bf16[64,1024]{1,0:T(8,128)(2,1)S(1)}, bf16[64,1024]{1,0:T(8,128)(2,1)}, u32[]{:S(2)}) copy-start(bf16[64,1024]{1,0:T(8,128)(2,1)} %all-reduce.3.cloned.1.call-done) | copy-start | bytes 393220 | tf_op jit(solution)/shard_map/while
  440.1 8.3 %collective-permute-start = (bf16[64,2048]{1,0:T(8,128)(2,1)S(1)}, bf16[64,2048]{1,0:T(8,128)(2,1)S(1)}, u32[]{:S(2)}, u32[]{:S(2)}) collective-permute-start(bf16[64,2048]{1,0:T(8,128)(2,1)S(1)} %get-tuple-element.364), channel_id=1, source_target_pairs={{16,0},{17,1},{18,2},{19,3},{20,4},{21,5},{22,6},{23,7},{24,8},{25... | collective-permute-start | bytes 786440 | tf_op jit(solution)/shard_map/while/body/eval_jaxpr/ppermute | solution.py:12
  448.3 22.7 %copy-start.1 = (bf16[128,2048]{1,0:T(8,128)(2,1)}, bf16[128,2048]{1,0:T(8,128)(2,1)S(1)}, u32[]{:S(2)}) copy-start(bf16[128,2048]{1,0:T(8,128)(2,1)S(1)} %get-tuple-element.261) | copy-start | bytes 1572868
  448.3 29.6 %copy-start.3 = (bf16[128,2048]{1,0:T(8,128)(2,1)}, bf16[128,2048]{1,0:T(8,128)(2,1)S(1)}, u32[]{:S(2)}) copy-start(bf16[128,2048]{1,0:T(8,128)(2,1)S(1)} %get-tuple-element.259) | copy-start | bytes 1572868
  448.3 26.1 %all-gather.11.cloned.1.call-start = ((), (), s32[]{:S(2)}) async-start(), calls=%async_computation.2 | async-start | bytes 1572864 | tf_op jit(solution)/shard_map/all_gather | solution.py:90
  449.1 47.3 %all-gather.13.cloned.1.call-start = ((), (), s32[]{:S(2)}) async-start(), calls=%async_computation.3 | async-start | bytes 1572864 | tf_op jit(solution)/shard_map/all_gather | solution.py:91
Sparse Core Ops, SparseCore 0:
  9.5 59.4 all-gather.6
  70.6 56.7 all-gather.8
  132.1 17.8 all-reduce.2
  154.0 72.1 all-reduce.4
  240.1 16.1 all-reduce.2
  260.4 72.2 all-reduce.4
  346.5 16.1 all-reduce.2
  366.7 72.2 all-reduce.4
  450.7 23.6 all-gather.10
  476.4 19.9 all-gather.12
where the time goes:
time: 510 us
  waiting for transfers between devices  428 us (84%)
  matrix products  31.4 us (6%)
  blocking collectives  20.7 us (4%)
  between operations  14.2 us (3%)
  other arithmetic  10.8 us (2%)
    psum x3, waiting for transfers between devices, advance(): total = lax.psum(branch.astype(jnp.bfloat16), 'dp').astype(jnp.float32)  217 us
    all_gather x1, waiting for transfers between devices, body(): lax.all_gather(w_out, 'section', axis=1, tiled=True)  60.3 us
    all_gather x1, waiting for transfers between devices, body(): lax.all_gather(w_in, 'section', axis=1, tiled=True)  58.3 us
    psum x3, waiting for transfers between devices, advance(): lax.psum(partial_value.astype(jnp.bfloat16), 'mp').astype(jnp.float32)  50.6 us
    ppermute x3, waiting for transfers between devices, shifted(): return lax.ppermute(value, axis, pairs)  20.4 us
    all_gather x1, waiting for transfers between devices, body(): lax.all_gather(dys[None], 'section', axis=0, tiled=True)  15.6 us
    dot_general x3, matrix products, advance(): lax.dot_general(upper, out_rows, (((1,), (1,)), ((), ())), preferred_elem...  12.7 us
    all_gather x1, blocking collectives, body(): lax.all_gather(gees[None], 'section', axis=0, tiled=True)  12.7 us
  transfers between devices with their start and end apart: 13, of which 13 were waited for; matrix products, arithmetic and copies ran while one was open for 2% of the time, Pallas kernels for 0%

commit v1 on v0

--- a/solution.py
+++ b/solution.py
@@ -2,6 +2,7 @@
 import jax.numpy as jnp
 from jax import lax
 from jax.sharding import PartitionSpec as P
+from jax.lax import all_to_all, axis_size
 
 MICRO = 2
 
@@ -34,9 +35,14 @@
     tok_rows = out_grad.shape[0]
     block = tok_rows // MICRO
     width = out_grad.shape[1]
+
+    def record_register(sheet, along_axis):
+        state_now = jnp.concatenate([sheet] * axis_size(along_axis), axis=1)
+        return all_to_all(state_now, along_axis, split_axis=1, concat_axis=1, tiled=True)
+
     full_in, full_out = (
         lax.all_gather(w_in, "section", axis=1, tiled=True),
-        lax.all_gather(w_out, "section", axis=1, tiled=True),
+        record_register(w_out, "section"),
     )
     units = full_in.shape[1] * full_in.shape[2]
     per_block = full_in.shape[2]

time: 510 us -> 496 us (0.973)
  waiting for transfers between devices: 428 us -> 403 us
  starting transfers between devices: 4.17 us -> 9.86 us
    all_to_all x0 -> x1, waiting for transfers between devices: none -> 92.9 us  [record_register(): all_to_all(state_now, along_axis, split_axis=1, concat_axis=1, tiled=True)]
    all_gather x1 -> x0, waiting for transfers between devices: 60.3 us -> none  [body(): lax.all_gather(w_out, 'section', axis=1, tiled=True)]
    all_gather x1, waiting for transfers between devices: 58.3 us -> 1.07 us  [body(): lax.all_gather(w_in, 'section', axis=1, tiled=True)]
    all_to_all x0 -> x1, starting transfers between devices: none -> 5.73 us  [record_register(): all_to_all(state_now, along_axis, split_axis=1, concat_axis=1, tiled=True)]
  transfers between devices with their start and end apart: 13 -> 13, of which waited for: 13 -> 13; matrix products, arithmetic and copies ran while one was open for 2% -> 3% of each run, Pallas kernels for 0% -> 0%
where the time goes in v1:
time: 496 us; the launch traced here: 495 us
  waiting for transfers between devices  403 us (81%)
  matrix products  31.4 us (6%)
  blocking collectives  20.7 us (4%)
  other arithmetic  15.4 us (3%)
  between operations  13.9 us (3%)
  starting transfers between devices  9.86 us (2%)
    psum x3, waiting for transfers between devices, advance(): total = lax.psum(branch.astype(jnp.bfloat16), 'dp').astype(jnp.float32)  217 us
    all_to_all x1, waiting for transfers between devices, record_register(): all_to_all(state_now, along_axis, split_axis=1, concat_axis=1, tiled=True)  92.9 us
    psum x3, waiting for transfers between devices, advance(): lax.psum(partial_value.astype(jnp.bfloat16), 'mp').astype(jnp.float32)  51.2 us
    ppermute x3, waiting for transfers between devices, shifted(): return lax.ppermute(value, axis, pairs)  20.4 us
    all_gather x1, waiting for transfers between devices, body(): lax.all_gather(dys[None], 'section', axis=0, tiled=True)  15.7 us
    dot_general x3, matrix products, advance(): lax.dot_general(upper, out_rows, (((1,), (1,)), ((), ())), preferred_elem...  12.7 us
    all_gather x1, blocking collectives, body(): lax.all_gather(gees[None], 'section', axis=0, tiled=True)  12.7 us
    dot_general x3, matrix products, advance(): branch = jnp.dot(gee, in_rows, preferred_element_type=jnp.float32)  11.6 us
  transfers between devices with their start and end apart: 13, of which 13 were waited for; matrix products, arithmetic and copies ran while one was open for 3% of the time, Pallas kernels for 0%

profile of v1, /device:TPU:0, one launch (start us, length us, event | category | flops | bytes accessed | tf_op | source)
XLA Modules:
  0.0 494.9 jit_solution(4044905733619837821)
XLA Ops:
  7.2 0.0 all-gather.6.cloned.1.call-start
  7.2 0.7 all-gather.6.cloned.1.call-update
  7.9 4.6 pad_maximum_fusion
  12.5 5.7 %all-to-all-start = ((bf16[1,2,512,2048]{3,2,0,1:T(8,128)(2,1)}), bf16[1,2,512,2048]{3,2,0,1:T(8,128)(2,1)}, u32[]{:S(2)}, u32[]{:S(2)}) async-start(bf16[1,2,512,2048]{3,2,0,1:T(8,128)(2,1)} %pad_maximum_fusion), calls=%async_computation | async-start | bytes 8388608 | tf_op jit(solution)/shard_map/all_to_all | solution.py:41
  18.3 92.9 %all-to-all-done = bf16[1,2,512,2048]{3,2,0,1:T(8,128)(2,1)} async-done(((bf16[1,2,512,2048]{3,2,0,1:T(8,128)(2,1)}), bf16[1,2,512,2048]{3,2,0,1:T(8,128)(2,1)}, u32[]{:S(2)}, u32[]{:S(2)}) %all-to-all-start) | async-done | bytes 4194336 | tf_op jit(solution)/shard_map/all_to_all | solution.py:41
  111.1 1.1 all-gather.6.cloned.1.call-done
  112.4 0.0 copy-done.2
  112.4 0.0 copy-done.4
  112.4 321.4 %while.21 = (s32[]{:T(128)}, bf16[64,2048]{1,0:T(8,128)(2,1)S(1)}, bf16[128,2048]{1,0:T(8,128)(2,1)S(1)}, bf16[128,1024]{1,0:T(8,128)(2,1)S(1)}, bf16[128,2048]{...) while((s32[]{:T(128)}, bf16[64,2048]{1,0:T(8,128)(2,1)S(1)}, ...), condition=%wide.region_3.4_spmd, body=%wide.region_0.3_spmd.sunk | while | flops 539820032 | bytes 16384420 | solution.py:88
  112.4 0.0 all-reduce.3.cloned.1.call-start
  112.5 0.1 select_dynamic-update-slice_fusion.6
  112.6 4.2 convolution_convert_fusion.8
  116.8 0.0 all-reduce.3.cloned.1.call-update
  116.9 0.0 all-reduce.5.cloned.1.call-start
  116.9 18.6 %all-reduce.3.cloned.1.call-done = bf16[64,1024]{1,0:T(8,128)(2,1)} async-done(((bf16[64,1024]{1,0:T(8,128)(2,1)}), bf16[64,1024]{1,0:T(8,128)(2,1)}) %all-reduce.3.cloned.1.call-update) | async-done | bytes 131088 | tf_op jit(solution)/shard_map/while/body/eval_jaxpr/psum | solution.py:65
  135.5 3.9 convolution_convert_fusion.9
  139.4 0.0 all-reduce.5.cloned.1.call-update
  139.4 72.4 %all-reduce.5.cloned.1.call-done = bf16[64,2048]{1,0:T(8,128)(2,1)} async-done(((bf16[64,2048]{1,0:T(8,128)(2,1)}), bf16[64,2048]{1,0:T(8,128)(2,1)}) %all-reduce.5.cloned.1.call-update) | async-done | bytes 262160 | tf_op jit(solution)/shard_map/while/body/eval_jaxpr/psum | solution.py:69
  211.8 1.1 select_dynamic-update-slice_fusion.7
  212.9 1.3 collective-permute-start
  214.2 0.0 copy-done
  214.2 0.2 select_dynamic-update-slice_fusion.8
  214.3 6.8 %collective-permute-done = bf16[64,2048]{1,0:T(8,128)(2,1)S(1)} collective-permute-done((bf16[64,2048]{1,0:T(8,128)(2,1)S(1)}, bf16[64,2048]{1,0:T(8,128)(2,1)S(1)}, u32[]{:S(2)}, u32[]{:S(2)}) %collective-permute-start) | collective-permute-done | bytes 262176 | tf_op jit(solution)/shard_map/while/body/eval_jaxpr/ppermute | solution.py:13
  221.1 0.0 all-reduce.3.cloned.1.call-start
  221.1 0.1 select_dynamic-update-slice_fusion.6
  221.3 4.2 convolution_convert_fusion.8
  225.5 0.0 all-reduce.3.cloned.1.call-update
  225.5 0.0 all-reduce.5.cloned.1.call-start
  225.6 16.3 %all-reduce.3.cloned.1.call-done = bf16[64,1024]{1,0:T(8,128)(2,1)} async-done(((bf16[64,1024]{1,0:T(8,128)(2,1)}), bf16[64,1024]{1,0:T(8,128)(2,1)}) %all-reduce.3.cloned.1.call-update) | async-done | bytes 131088 | tf_op jit(solution)/shard_map/while/body/eval_jaxpr/psum | solution.py:65
  241.9 3.9 convolution_convert_fusion.9
  245.7 0.0 all-reduce.5.cloned.1.call-update
  245.8 72.4 %all-reduce.5.cloned.1.call-done = bf16[64,2048]{1,0:T(8,128)(2,1)} async-done(((bf16[64,2048]{1,0:T(8,128)(2,1)}), bf16[64,2048]{1,0:T(8,128)(2,1)}) %all-reduce.5.cloned.1.call-update) | async-done | bytes 262160 | tf_op jit(solution)/shard_map/while/body/eval_jaxpr/psum | solution.py:69
  318.1 1.1 select_dynamic-update-slice_fusion.7
  319.2 1.3 collective-permute-start
  320.5 0.2 select_dynamic-update-slice_fusion.8
  320.7 6.8 %collective-permute-done = bf16[64,2048]{1,0:T(8,128)(2,1)S(1)} collective-permute-done((bf16[64,2048]{1,0:T(8,128)(2,1)S(1)}, bf16[64,2048]{1,0:T(8,128)(2,1)S(1)}, u32[]{:S(2)}, u32[]{:S(2)}) %collective-permute-start) | collective-permute-done | bytes 262176 | tf_op jit(solution)/shard_map/while/body/eval_jaxpr/ppermute | solution.py:13
  327.5 0.1 select_dynamic-update-slice_fusion.6
  327.6 4.2 convolution_convert_fusion.8
  331.8 0.0 all-reduce.3.cloned.1.call-update
  331.9 0.0 all-reduce.5.cloned.1.call-start
  331.9 16.3 %all-reduce.3.cloned.1.call-done = bf16[64,1024]{1,0:T(8,128)(2,1)} async-done(((bf16[64,1024]{1,0:T(8,128)(2,1)}), bf16[64,1024]{1,0:T(8,128)(2,1)}) %all-reduce.3.cloned.1.call-update) | async-done | bytes 131088 | tf_op jit(solution)/shard_map/while/body/eval_jaxpr/psum | solution.py:65
  348.2 3.9 convolution_convert_fusion.9
  352.1 0.0 all-reduce.5.cloned.1.call-update
  352.1 72.4 %all-reduce.5.cloned.1.call-done = bf16[64,2048]{1,0:T(8,128)(2,1)} async-done(((bf16[64,2048]{1,0:T(8,128)(2,1)}), bf16[64,2048]{1,0:T(8,128)(2,1)}) %all-reduce.5.cloned.1.call-update) | async-done | bytes 262160 | tf_op jit(solution)/shard_map/while/body/eval_jaxpr/psum | solution.py:69
  424.4 1.1 select_dynamic-update-slice_fusion.7
  425.5 1.3 collective-permute-start
  426.8 0.2 select_dynamic-update-slice_fusion.8
  427.0 6.8 %collective-permute-done = bf16[64,2048]{1,0:T(8,128)(2,1)S(1)} collective-permute-done((bf16[64,2048]{1,0:T(8,128)(2,1)S(1)}, bf16[64,2048]{1,0:T(8,128)(2,1)S(1)}, u32[]{:S(2)}, u32[]{:S(2)}) %collective-permute-start) | collective-permute-done | bytes 262176 | tf_op jit(solution)/shard_map/while/body/eval_jaxpr/ppermute | solution.py:13
  433.8 0.0 all-gather.8.cloned.1.call-start
  433.8 0.7 all-gather.8.cloned.1.call-update
  434.5 0.0 all-gather.10.cloned.1.call-start
  434.6 1.1 fusion.10
  435.7 8.1 %all_gather.18 = bf16[2,128,1024]{2,1,0:T(8,128)(2,1)S(1)} all-gather(bf16[1,128,1024]{2,1,0:T(8,128)(2,1)S(1)} %fusion.10), channel_id=1, replica_groups=mesh['section'=2,'dp'=8,'mp'=2] {'section'}, dimensions={0}, use_global_device_ids=true | all-gather | bytes 786432 | tf_op jit(solution)/shard_map/all_gather | solution.py:99
  443.8 12.7 %all-gather = bf16[256,1024]{1,0:T(8,128)(2,1)S(1)} all-gather(bf16[128,1024]{1,0:T(8,128)(2,1)S(1)} %get-tuple-element.260), channel_id=2, replica_groups=mesh['section'=2,'dp'=8,'mp'=2] {'section'}, dimensions={0}, use_global_device_ids=true | all-gather | bytes 786432 | tf_op jit(solution)/shard_map/all_gather | solution.py:98
  456.5 0.0 copy-done.1
  456.5 0.0 all-gather.10.cloned.1.call-update
  456.6 3.3 all-gather.8.cloned.1.call-done
  459.9 1.8 convolution_convert_fusion.4
  461.6 1.8 convolution_convert_fusion.5
  463.4 2.8 add_bitcast_fusion.1
  466.2 15.7 %all-gather.10.cloned.1.call-done = bf16[256,2048]{1,0:T(8,128)(2,1)} async-done(((bf16[128,2048]{1,0:T(8,128)(2,1)}), bf16[256,2048]{1,0:T(8,128)(2,1)}) %all-gather.10.cloned.1.call-update) | async-done | bytes 1048592 | tf_op jit(solution)/shard_map/all_gather | solution.py:97
  482.0 1.8 convolution_convert_fusion.2
  483.8 1.8 convolution_convert_fusion.3
  485.5 2.8 add_bitcast_fusion
  (17 shorter events, 0.2 us)
Async XLA Ops:
  7.2 105.0 %all-gather.6.cloned.1.call-start = ((), (), s32[]{:S(2)}) async-start(), calls=%async_computation.1 | async-start | bytes 6291456 | tf_op jit(solution)/shard_map/all_gather | solution.py:44
  12.5 99.9 %copy-start.2 = (bf16[1,128,1024]{2,1,0:T(8,128)(2,1)S(1)}, bf16[1,128,1024]{2,1,0:T(8,128)(2,1)}, u32[]{:S(2)}) copy-start(bf16[1,128,1024]{2,1,0:T(8,128)(2,1)} %param.8) | copy-start | bytes 786436
  12.5 99.9 %copy-start.4 = (bf16[128,2048]{1,0:T(8,128)(2,1)S(1)}, bf16[128,2048]{1,0:T(8,128)(2,1)}, u32[]{:S(2)}) copy-start(bf16[128,2048]{1,0:T(8,128)(2,1)} %param.9) | copy-start | bytes 1572868
  12.5 98.6 %all-to-all-start = ((bf16[1,2,512,2048]{3,2,0,1:T(8,128)(2,1)}), bf16[1,2,512,2048]{3,2,0,1:T(8,128)(2,1)}, u32[]{:S(2)}, u32[]{:S(2)}) async-start(bf16[1,2,512,2048]{3,2,0,1:T(8,128)(2,1)} %pad_maximum_fusion), calls=%async_computation | async-start | bytes 8388608 | tf_op jit(solution)/shard_map/all_to_all | solution.py:41
  112.4 23.1 %all-reduce.3.cloned.1.call-start = ((), (), s32[]{:S(2)}) async-start(), calls=%async_computation.4 | async-start | bytes 262144 | tf_op jit(solution)/shard_map/while/body/eval_jaxpr/psum | solution.py:65
  116.9 94.9 %all-reduce.5.cloned.1.call-start = ((), (), s32[]{:S(2)}) async-start(), calls=%async_computation.5 | async-start | bytes 524288 | tf_op jit(solution)/shard_map/while/body/eval_jaxpr/psum | solution.py:69
  135.5 78.6 %copy-start = (bf16[64,1024]{1,0:T(8,128)(2,1)S(1)}, bf16[64,1024]{1,0:T(8,128)(2,1)}, u32[]{:S(2)}) copy-start(bf16[64,1024]{1,0:T(8,128)(2,1)} %all-reduce.3.cloned.1.call-done) | copy-start | bytes 393220 | tf_op jit(solution)/shard_map/while
  212.9 8.3 %collective-permute-start = (bf16[64,2048]{1,0:T(8,128)(2,1)S(1)}, bf16[64,2048]{1,0:T(8,128)(2,1)S(1)}, u32[]{:S(2)}, u32[]{:S(2)}) collective-permute-start(bf16[64,2048]{1,0:T(8,128)(2,1)S(1)} %get-tuple-element.364), channel_id=1, source_target_pairs={{16,0},{17,1},{18,2},{19,3},{20,4},{21,5},{22,6},{23,7},{24,8},{25... | collective-permute-start | bytes 786440 | tf_op jit(solution)/shard_map/while/body/eval_jaxpr/ppermute | solution.py:13
  221.1 20.8 %all-reduce.3.cloned.1.call-start = ((), (), s32[]{:S(2)}) async-start(), calls=%async_computation.4 | async-start | bytes 262144 | tf_op jit(solution)/shard_map/while/body/eval_jaxpr/psum | solution.py:65
  225.5 92.6 %all-reduce.5.cloned.1.call-start = ((), (), s32[]{:S(2)}) async-start(), calls=%async_computation.5 | async-start | bytes 524288 | tf_op jit(solution)/shard_map/while/body/eval_jaxpr/psum | solution.py:69
  241.9 78.6 %copy-start = (bf16[64,1024]{1,0:T(8,128)(2,1)S(1)}, bf16[64,1024]{1,0:T(8,128)(2,1)}, u32[]{:S(2)}) copy-start(bf16[64,1024]{1,0:T(8,128)(2,1)} %all-reduce.3.cloned.1.call-done) | copy-start | bytes 393220 | tf_op jit(solution)/shard_map/while
  319.2 8.3 %collective-permute-start = (bf16[64,2048]{1,0:T(8,128)(2,1)S(1)}, bf16[64,2048]{1,0:T(8,128)(2,1)S(1)}, u32[]{:S(2)}, u32[]{:S(2)}) collective-permute-start(bf16[64,2048]{1,0:T(8,128)(2,1)S(1)} %get-tuple-element.364), channel_id=1, source_target_pairs={{16,0},{17,1},{18,2},{19,3},{20,4},{21,5},{22,6},{23,7},{24,8},{25... | collective-permute-start | bytes 786440 | tf_op jit(solution)/shard_map/while/body/eval_jaxpr/ppermute | solution.py:13
  327.5 20.8 %all-reduce.3.cloned.1.call-start = ((), (), s32[]{:S(2)}) async-start(), calls=%async_computation.4 | async-start | bytes 262144 | tf_op jit(solution)/shard_map/while/body/eval_jaxpr/psum | solution.py:65
  331.9 92.6 %all-reduce.5.cloned.1.call-start = ((), (), s32[]{:S(2)}) async-start(), calls=%async_computation.5 | async-start | bytes 524288 | tf_op jit(solution)/shard_map/while/body/eval_jaxpr/psum | solution.py:69
  348.2 78.6 %copy-start = (bf16[64,1024]{1,0:T(8,128)(2,1)S(1)}, bf16[64,1024]{1,0:T(8,128)(2,1)}, u32[]{:S(2)}) copy-start(bf16[64,1024]{1,0:T(8,128)(2,1)} %all-reduce.3.cloned.1.call-done) | copy-start | bytes 393220 | tf_op jit(solution)/shard_map/while
  425.5 8.3 %collective-permute-start = (bf16[64,2048]{1,0:T(8,128)(2,1)S(1)}, bf16[64,2048]{1,0:T(8,128)(2,1)S(1)}, u32[]{:S(2)}, u32[]{:S(2)}) collective-permute-start(bf16[64,2048]{1,0:T(8,128)(2,1)S(1)} %get-tuple-element.364), channel_id=1, source_target_pairs={{16,0},{17,1},{18,2},{19,3},{20,4},{21,5},{22,6},{23,7},{24,8},{25... | collective-permute-start | bytes 786440 | tf_op jit(solution)/shard_map/while/body/eval_jaxpr/ppermute | solution.py:13
  433.8 22.7 %copy-start.1 = (bf16[128,2048]{1,0:T(8,128)(2,1)}, bf16[128,2048]{1,0:T(8,128)(2,1)S(1)}, u32[]{:S(2)}) copy-start(bf16[128,2048]{1,0:T(8,128)(2,1)S(1)} %get-tuple-element.261) | copy-start | bytes 1572868
  433.8 29.6 %copy-start.3 = (bf16[128,2048]{1,0:T(8,128)(2,1)}, bf16[128,2048]{1,0:T(8,128)(2,1)S(1)}, u32[]{:S(2)}) copy-start(bf16[128,2048]{1,0:T(8,128)(2,1)S(1)} %get-tuple-element.259) | copy-start | bytes 1572868
  433.8 26.1 %all-gather.8.cloned.1.call-start = ((), (), s32[]{:S(2)}) async-start(), calls=%async_computation.2 | async-start | bytes 1572864 | tf_op jit(solution)/shard_map/all_gather | solution.py:96
  434.5 47.5 %all-gather.10.cloned.1.call-start = ((), (), s32[]{:S(2)}) async-start(), calls=%async_computation.3 | async-start | bytes 1572864 | tf_op jit(solution)/shard_map/all_gather | solution.py:97
Sparse Core Ops, SparseCore 0:
  9.5 102.6 all-gather.5
  117.0 18.4 all-reduce.2
  139.5 72.2 all-reduce.4
  225.6 16.1 all-reduce.2
  245.9 72.1 all-reduce.4
  332.0 16.1 all-reduce.2
  352.2 72.1 all-reduce.4
  436.1 23.6 all-gather.7
  462.0 19.9 all-gather.9
